TPU v7x, 256 devices: a whole 4x4x8 slice. The times are simulated.
256 devices in a mesh: gx: 16 (over x_lo, y, core), gy: 16 (over z, x_hi).
Axes of the slice: x: 4 (x_hi: 2, x_lo: 2; x = x_hi * 2 + x_lo), y: 4, z: 8, core: 2. Of those that a mesh axis runs over, the one named last changes fastest.
Arguments:
- source: float32 [320, 320, 640], P('gx', 'gy'), may hold values from -210 to 210
- conductivity: float32 [320, 320, 640], P('gx', 'gy'), may hold values from 0.001 to 1
- absorption: float32 [320, 320, 640], P('gx', 'gy'), may hold values from 1 to 10
Outputs:
- solution: float32 [320, 320, 640], P('gx', 'gy')
- correction: float32 [192, 192, 384], P('gx', 'gy')
All inputs are finite; a program needn't handle non-finite values.
Results may differ from a plain program's by a relative error of at most 0.00023.
Values sent between devices are 32-bit elements; how exact they have to be, the bound alone decides.
A program may use at most 128 MiB of HBM per device.

v0:
```python
import functools
import math

import jax
import jax.numpy as jnp
import numpy as np
from jax import lax
from jax.experimental import pallas as pl
from jax.experimental.pallas import tpu as pltpu
from jax.sharding import PartitionSpec as P

MESH = pl.DeviceIdType.MESH
SWEEPS = 3
F32 = jnp.float32


def deriv_table(points):
    count = len(points)
    bary = [1.0 / np.prod([points[j] - points[k] for k in range(count) if k != j]) for j in range(count)]
    table = np.zeros((count, count))
    for i in range(count):
        for j in range(count):
            if i != j:
                table[i, j] = bary[j] / (bary[i] * (points[i] - points[j]))
        table[i, i] = -np.sum(table[i])
    return table


ROOT = math.sqrt(3.0 / 7.0)
WF = [0.1, 49.0 / 90.0, 32.0 / 45.0, 49.0 / 90.0, 0.1]
WC = [1.0 / 3.0, 4.0 / 3.0, 1.0 / 3.0]
DF = deriv_table(np.array([-1.0, -ROOT, 0.0, ROOT, 1.0]))
JA, JB, JC = (ROOT * ROOT + ROOT) / 2, 1 - ROOT * ROOT, (ROOT * ROOT - ROOT) / 2
JROWS = [[1.0, 0.0, 0.0], [JA, JB, JC], [0.0, 1.0, 0.0], [JC, JB, JA], [0.0, 0.0, 1.0]]


B00, B01 = (DF[4][4] + DF[0][4]) / 2, (DF[4][3] + DF[0][3]) / 2
B10, B11 = (DF[3][4] + DF[1][4]) / 2, (DF[3][3] + DF[1][3]) / 2
G00, G01 = (DF[4][4] - DF[0][4]) / 2, (DF[4][3] - DF[0][3]) / 2
G10, G11 = (DF[3][4] - DF[1][4]) / 2, (DF[3][3] - DF[1][3]) / 2
A0, A1 = DF[2][4], DF[2][3]


def stiff5(v, flux):
    a0, a1 = v[4] - v[0], v[3] - v[1]
    m2 = v[2] + v[2]
    s0, s1 = v[0] + v[4] - m2, v[1] + v[3] - m2
    p0, p1 = B00 * a0 + B01 * a1, B10 * a0 + B11 * a1
    q0, q1 = G00 * s0 + G01 * s1, G10 * s0 + G11 * s1
    f0, f4 = flux[0] * (p0 - q0), flux[4] * (p0 + q0)
    f1, f3 = flux[1] * (p1 - q1), flux[3] * (p1 + q1)
    f2 = flux[2] * (A0 * a0 + A1 * a1)
    sp0, sq0, sp1, sq1 = f4 + f0, f4 - f0, f3 + f1, f3 - f1
    b0 = A0 * f2 + B00 * sp0 + B10 * sp1
    b1 = A1 * f2 + B01 * sp0 + B11 * sp1
    c0, c1 = G00 * sq0 + G10 * sq1, G01 * sq0 + G11 * sq1
    mid = c0 + c1
    return [c0 - b0, c1 - b1, -(mid + mid), c1 + b1, c0 + b0]


DD = (DF * DF).T


def diag5(flux):
    s0, s1, d0, d1 = flux[0] + flux[4], flux[1] + flux[3], flux[0] - flux[4], flux[1] - flux[3]
    out = [None] * 5
    for r in (0, 1):
        even = (DD[r][0] + DD[r][4]) / 2 * s0 + (DD[r][1] + DD[r][3]) / 2 * s1 + DD[r][2] * flux[2]
        odd = (DD[r][0] - DD[r][4]) / 2 * d0 + (DD[r][1] - DD[r][3]) / 2 * d1
        out[r], out[4 - r] = even + odd, even - odd
    out[2] = DD[2][0] * s0 + DD[2][1] * s1
    return out


def stiff3(v, flux):
    a = 0.5 * (v[2] - v[0])
    s = v[0] + v[2] - (v[1] + v[1])
    f0, f1, f2 = flux[0] * (a - s), flux[1] * a, flux[2] * (a + s)
    b = 0.5 * (f0 + f1 + f2)
    t = f2 - f0
    return [t - b, -(t + t), t + b]


DC = deriv_table(np.array([-1.0, 0.0, 1.0]))
DDC = (DC * DC).T


def diag3(flux):
    s = flux[0] + flux[2]
    return [
        DDC[0][0] * flux[0] + DDC[0][1] * flux[1] + DDC[0][2] * flux[2],
        DDC[1][0] * s,
        DDC[2][0] * flux[0] + DDC[2][1] * flux[1] + DDC[2][2] * flux[2],
    ]


def restrict5(y):
    return [y[0] + JA * y[1] + JC * y[3], JB * (y[1] + y[3]) + y[2], y[4] + JC * y[1] + JA * y[3]]


def up(x):
    return pltpu.roll(x, 127, 1)


def down(x):
    return pltpu.roll(x, 1, 1)


def loop(count, body, unroll=1):
    def step(i, carry):
        body(i)
        return carry

    lax.fori_loop(0, count, step, 0, unroll=unroll)


class Level:
    def __init__(self, q, fxy, f0, fq, mass, inv):
        self.q, self.kz = q, q - 1
        self.fxy, self.f0, self.fq, self.mass, self.inv = fxy, f0, fq, mass, inv
        self.stiff, self.diag = (stiff5, diag5) if q == 5 else (stiff3, diag3)
        self.face = q * self.kz * 4
        self.loop = loop if q == 5 else (lambda n, body: [body(i) for i in range(n)])

    def at(self, i, j, k):
        return ((i * self.q + j) * self.kz + k) * 16

    def edge(self, i, j):
        return (i * self.q + j) * 16


def row(ref, start):
    if not isinstance(start, int):
        start = pl.multiple_of(start, 16)
    return ref[pl.ds(start, 16), :]


def put(ref, start, value):
    if not isinstance(start, int):
        start = pl.multiple_of(start, 16)
    ref[pl.ds(start, 16), :] = value


def element_rows():
    e = lax.broadcasted_iota(jnp.int32, (16, 128), 0)
    return e // 4, e % 4


def join_y(lo, hi):
    _, ey = element_rows()
    hi = hi + jnp.where(ey < 3, pltpu.roll(lo, 15, 0), 0.0)
    return jnp.where(ey > 0, pltpu.roll(hi, 1, 0), lo), hi


def join_x(lo, hi):
    ex, _ = element_rows()
    hi = hi + jnp.where(ex < 3, pltpu.roll(lo, 12, 0), 0.0)
    return jnp.where(ex > 0, pltpu.roll(hi, 4, 0), lo), hi


def join_planes_x(lv, out):
    q, kz = lv.q, lv.kz

    def body(j):
        for k in range(kz):
            lo, hi = join_x(row(out, lv.at(0, j, k)), row(out, lv.at(q - 1, j, k)))
            put(out, lv.at(0, j, k), lo)
            put(out, lv.at(q - 1, j, k), hi)

    lv.loop(q, body)


def join_planes_y(lv, out):
    q, kz = lv.q, lv.kz

    def body(i):
        for k in range(kz):
            lo, hi = join_y(row(out, lv.at(i, 0, k)), row(out, lv.at(i, q - 1, k)))
            put(out, lv.at(i, 0, k), lo)
            put(out, lv.at(i, q - 1, k), hi)

    lv.loop(q, body)


def apply_local(lv, out, u, scaled=None, sums=None, restrict=None, keep=True):
    q, kz = lv.q, lv.kz

    def along_z(i):
        total = None
        for j in range(q):
            base = lv.at(i, j, 0)
            if scaled is None:
                v = [row(u, base + 16 * k) for k in range(kz)]
            else:
                v = [row(scaled, base + 16 * k) * row(lv.inv, base + 16 * k) for k in range(kz)]
                for k in range(kz):
                    put(u, base + 16 * k, v[k])
                if sums is not None:
                    part = v[0] * v[0]
                    part = part + part
                    for k in range(1, kz):
                        part = part + v[k] * v[k]
                    total = part if total is None else total + part
            flux = [row(lv.f0, lv.edge(i, j))] + [row(lv.fxy, base + 16 * k) for k in range(1, kz)] + [row(lv.fq, lv.edge(i, j))]
            g = lv.stiff(v + [up(v[0])], flux)
            g = [g[0] + down(g[kz])] + g[1:kz]
            for k in range(kz):
                put(out, base + 16 * k, g[k] + row(lv.mass, base + 16 * k) * v[k])
        if sums is not None:
            sums[...] += total

    def along_x(j):
        for k in range(kz):
            places = [lv.at(i, j, k) for i in range(q)]
            g = lv.stiff([row(u, p) for p in places], [row(lv.fxy, p) for p in places])
            for i in range(q):
                put(out, places[i], row(out, places[i]) + g[i])

    def along_y(i):
        for k in range(kz):
            places = [lv.at(i, j, k) for j in range(q)]
            g = lv.stiff([row(u, p) for p in places], [row(lv.fxy, p) for p in places])
            g = [row(out, places[j]) + g[j] for j in range(q)]
            if restrict is not None:
                c = restrict5(g)
                for jc in range(3):
                    put(restrict, ((i * 3 + jc) * 4 + k) * 16, c[jc])
            if keep:
                g[0], g[q - 1] = join_y(g[0], g[q - 1])
                for j in range(q):
                    put(out, places[j], g[j])

    if sums is not None:
        sums[...] = jnp.zeros_like(sums)
    lv.loop(q, along_z)
    lv.loop(q, along_x)
    lv.loop(q, along_y)
    if keep:
        join_planes_x(lv, out)


def sum_squares(lv, scaled, sums):
    sums[...] = jnp.zeros_like(sums)

    def body(i):
        total = None
        for j in range(lv.q):
            for k in range(lv.kz):
                p = lv.at(i, j, k)
                v = row(scaled, p) * row(lv.inv, p)
                v = v * v
                if k == 0:
                    v = v + v
                total = v if total is None else total + v
        sums[...] += total

    lv.loop(lv.q, body)


def restrict_xz(lc, tmp, out):
    for jc in range(3):
        cols = [restrict5([row(tmp, ((i * 3 + jc) * 4 + k) * 16) for i in range(5)]) for k in range(4)]
        for ic in range(3):
            y = [cols[k][ic] for k in range(4)]
            first = y[0] + JA * y[1] + JC * y[3] + down(JC * y[1] + JA * y[3])
            put(out, lc.at(ic, jc, 0), first)
            put(out, lc.at(ic, jc, 1), JB * (y[1] + y[3]) + y[2])
    join_planes_y(lc, out)
    join_planes_x(lc, out)


def restrict_y(lv, src, tmp):
    def body(i):
        for k in range(4):
            c = restrict5([row(src, lv.at(i, j, k)) for j in range(5)])
            for jc in range(3):
                put(tmp, ((i * 3 + jc) * 4 + k) * 16, c[jc])

    loop(5, body)


def local_diag(lv, out):
    q, kz = lv.q, lv.kz

    def along_z(i):
        for j in range(q):
            base = lv.at(i, j, 0)
            flux = [row(lv.f0, lv.edge(i, j))] + [row(lv.fxy, base + 16 * k) for k in range(1, kz)] + [row(lv.fq, lv.edge(i, j))]
            g = lv.diag(flux)
            g = [g[0] + down(g[kz])] + g[1:kz]
            for k in range(kz):
                put(out, base + 16 * k, g[k] + row(lv.mass, base + 16 * k))

    def along_x(j):
        for k in range(kz):
            places = [lv.at(i, j, k) for i in range(q)]
            g = lv.diag([row(lv.fxy, p) for p in places])
            for i in range(q):
                put(out, places[i], row(out, places[i]) + g[i])

    def along_y(i):
        for k in range(kz):
            places = [lv.at(i, j, k) for j in range(q)]
            g = lv.diag([row(lv.fxy, p) for p in places])
            g = [row(out, places[j]) + g[j] for j in range(q)]
            g[0], g[q - 1] = join_y(g[0], g[q - 1])
            for j in range(q):
                put(out, places[j], g[j])

    lv.loop(q, along_z)
    lv.loop(q, along_x)
    lv.loop(q, along_y)
    join_planes_x(lv, out)


DIRS = [(0, 1), (0, -1), (1, 0), (-1, 0), (1, 1), (1, -1), (-1, 1), (-1, -1)]


class Exchange:
    def __init__(self, round_index, fields, offsets, bufs, sems, ids):
        self.r, self.fields, self.ids = round_index, fields, ids
        self.face0, self.corner0 = offsets
        self.face_rows = sum(lv.face for lv, _ in fields)
        self.corner_rows = 8 * len(fields)
        self.bufs, self.sems = bufs, sems
        self.copies = []

    def pack(self):
        sface, scorner = self.bufs[0], self.bufs[2]
        at = self.face0
        for f, (lv, ref) in enumerate(self.fields):
            q, kz = lv.q, lv.kz
            for d, (dx, dy) in enumerate(DIRS[:4]):
                if dy:
                    j, first = (q - 1, 3) if dy > 0 else (0, 0)
                    for i in range(q):
                        for h in range(0, 4 * kz, 8):
                            sface[d, pl.ds(at + i * 4 * kz + h, 8), :] = ref[pl.ds(lv.at(i, j, 0) + first + 4 * h, 8, 4), :]
                else:
                    i = q - 1 if dx > 0 else 0
                    low = lax.broadcasted_iota(jnp.int32, (8, 128), 0) < 4
                    for m in range(0, q * kz, 2):
                        p = lv.at(i, 0, 0) + m * 16
                        if dx > 0:
                            one, two = ref[pl.ds(p + 8, 8), :], ref[pl.ds(p + 24, 8), :]
                            both = jnp.where(low, pltpu.roll(one, 4, 0), two)
                        else:
                            one, two = ref[pl.ds(p, 8), :], ref[pl.ds(p + 16, 8), :]
                            both = jnp.where(low, one, pltpu.roll(two, 4, 0))
                        sface[d, pl.ds(at + m * 4, 8), :] = both
            for c, (dx, dy) in enumerate(DIRS[4:]):
                p = lv.at(q - 1 if dx > 0 else 0, q - 1 if dy > 0 else 0, 0) + (12 if dx > 0 else 0) + (3 if dy > 0 else 0)
                for k in range(kz):
                    scorner[c, pl.ds(self.corner0 + f * 8 + k, 1), :] = ref[pl.ds(p + 16 * k, 1), :]
            at += lv.face

    def send(self):
        sface, rface, scorner, rcorner = self.bufs
        send_sem, recv_sem = self.sems
        x, y, nx, ny = self.ids
        for d, (dx, dy) in enumerate(DIRS):
            if d < 4:
                part = (d, pl.ds(self.face0, self.face_rows), slice(None))
                src, dst = sface.at[part], rface.at[part]
            else:
                part = (d - 4, pl.ds(self.corner0, self.corner_rows), slice(None))
                src, dst = scorner.at[part], rcorner.at[part]
            copy = pltpu.make_async_remote_copy(
                src_ref=src,
                dst_ref=dst,
                send_sem=send_sem.at[self.r, d],
                recv_sem=recv_sem.at[self.r, d],
                device_id=(lax.rem(x + dx + nx, nx), lax.rem(y + dy + ny, ny)),
                device_id_type=MESH,
            )
            copy.start()
            self.copies.append(copy)

    def start(self):
        self.pack()
        self.send()

    def finish(self):
        for copy in self.copies:
            copy.wait_recv()
        rface, rcorner = self.bufs[1], self.bufs[3]
        at = self.face0
        for f, (lv, ref) in enumerate(self.fields):
            q, kz = lv.q, lv.kz
            for d, (dx, dy) in enumerate(DIRS[:4]):
                if dy:
                    j, first = (0, 0) if dy > 0 else (q - 1, 3)
                    for i in range(q):
                        for h in range(0, 4 * kz, 8):
                            place = pl.ds(lv.at(i, j, 0) + first + 4 * h, 8, 4)
                            ref[place, :] = ref[place, :] + rface[d, pl.ds(at + i * 4 * kz + h, 8), :]
                else:
                    i = 0 if dx > 0 else q - 1
                    low = lax.broadcasted_iota(jnp.int32, (8, 128), 0) < 4
                    for m in range(0, q * kz, 2):
                        p = lv.at(i, 0, 0) + m * 16
                        both = rface[d, pl.ds(at + m * 4, 8), :]
                        turned = pltpu.roll(both, 4, 0)
                        if dx > 0:
                            a, b = pl.ds(p, 8), pl.ds(p + 16, 8)
                            ref[a, :] = ref[a, :] + jnp.where(low, both, 0.0)
                            ref[b, :] = ref[b, :] + jnp.where(low, turned, 0.0)
                        else:
                            a, b = pl.ds(p + 8, 8), pl.ds(p + 24, 8)
                            ref[a, :] = ref[a, :] + jnp.where(low, 0.0, turned)
                            ref[b, :] = ref[b, :] + jnp.where(low, 0.0, both)
            for c, (dx, dy) in enumerate(DIRS[4:]):
                p = lv.at(0 if dx > 0 else q - 1, 0 if dy > 0 else q - 1, 0) + (0 if dx > 0 else 12) + (0 if dy > 0 else 3)
                for k in range(kz):
                    place = pl.ds(p + 16 * k, 1)
                    ref[place, :] = ref[place, :] + rcorner[c, pl.ds(self.corner0 + f * 8 + k, 1), :]
            at += lv.face

    def wait_sent(self):
        for copy in self.copies:
            copy.wait_send()


class Lanes:
    def __init__(self, q):
        self.q = q
        step = {k: (k - 128) % q for k in range(q)}
        shift = {0: 0}
        k = 0
        for _ in range(q - 1):
            shift[step[k]] = shift[k] + self.begin(k, 1) - self.begin(step[k], 0)
            k = step[k]
        self.shift = [shift[k] % 128 for k in range(q)]
        lane = lax.broadcasted_iota(jnp.int32, (8, 128), 1)
        self.lane = lane
        self.split_index, self.merge_index = [], []
        for t in range(q):
            place = 128 * t + lane
            k = lax.rem(place, q)
            ez = lax.div(place, q)
            moved = ez
            for node in range(q):
                moved = jnp.where(k == node, ez + self.shift[node], moved)
            self.merge_index.append(jnp.bitwise_and(moved, 127))
            index = jnp.zeros((8, 128), jnp.int32)
            for node in range(q):
                ez = jnp.bitwise_and(lane - self.shift[node] + 128, 127)
                index = jnp.where(self.inside(node, t), q * ez + node - 128 * t, index)
            self.split_index.append(index)

    def begin(self, k, t):
        return -((k - 128 * t) // self.q)

    def inside(self, k, t):
        lo, hi = (self.begin(k, t) + self.shift[k]) % 128, (self.begin(k, t + 1) + self.shift[k]) % 128
        if lo < hi:
            return (self.lane >= lo) & (self.lane < hi) if lo else self.lane < hi
        return (self.lane >= lo) | (self.lane < hi) if hi else self.lane >= lo

    @staticmethod
    def gather(x, index):
        numbers = lax.GatherDimensionNumbers(
            offset_dims=(), collapsed_slice_dims=(1,), start_index_map=(1,), operand_batching_dims=(0,), start_indices_batching_dims=(0,)
        )
        return lax.gather(x, index[..., None], numbers, slice_sizes=(1, 1), mode=lax.GatherScatterMode.PROMISE_IN_BOUNDS)

    def split(self, stored):
        moved = [self.gather(stored[t], self.split_index[t]) for t in range(self.q)]
        out = []
        for k in range(self.q):
            x = moved[0]
            for t in range(1, self.q):
                x = jnp.where(self.inside(k, t), moved[t], x)
            out.append(pltpu.roll(x, (128 - self.shift[k]) % 128, 1) if self.shift[k] else x)
        return out

    def merge(self, nodes):
        moved = [pltpu.roll(nodes[k], self.shift[k], 1) if self.shift[k] else nodes[k] for k in range(self.q)]
        out = []
        for t in range(self.q):
            x = moved[0]
            for k in range(1, self.q):
                x = jnp.where(self.inside(k, t), moved[k], x)
            out.append(self.gather(x, self.merge_index[t]))
        return out


def pick(i, values):
    out = jnp.asarray(values[-1], F32)
    for n in range(len(values) - 2, -1, -1):
        out = jnp.where(i == n, jnp.asarray(values[n], F32), out)
    return out


def load_field(lanes, raw, store):
    def body(i):
        wx = pick(i, WF)
        for j in range(5):
            halves = []
            for h in range(2):
                stored = []
                for t in range(5):
                    low = raw[t, 10 * h + i, pl.ds(j, 4, 5), :]
                    high = raw[t, 10 * h + 5 + i, pl.ds(j, 4, 5), :]
                    stored.append(jnp.concatenate([low, high], axis=0))
                halves.append(lanes.split(stored))
            planes = [jnp.concatenate([halves[0][k], halves[1][k]], axis=0) * (wx * (WF[j] * WF[k])) for k in range(5)]
            store(i, j, planes)

    loop(5, body)


FR, CR, ER, CER = 1600, 288, 400, 144


def cheb_weights():
    sigma, rho = 5.0 / 3.0, 0.6
    theta, delta = 0.75, 0.45
    d = np.array([1.0 / theta, 0.0, 0.0])
    x = np.zeros(3)
    for sweep in range(SWEEPS):
        x = x + d
        if sweep + 1 < SWEEPS:
            nxt = 1.0 / (2.0 * sigma - rho)
            res = np.array([1.0, 0.0, 0.0]) - np.concatenate([[0.0], x[:-1]])
            d = nxt * rho * d + 2.0 * nxt / delta * res
            rho = nxt
    return [float(c) for c in x]


CHEB = cheb_weights()

ROUNDS = [(1, 1), (1, 1), (1, 1), (1, 1), (1, 1), (1, 1), (0, 1), (0, 1), (0, 1)]


def round_offsets():
    face, corner, out = 0, 0, []
    for fine, coarse in ROUNDS:
        out.append((face, corner))
        face += 80 * fine + 24 * coarse
        corner += 8 * (fine + coarse)
    return out, face, corner


OFFSETS, FACE_ROWS, CORNER_ROWS = round_offsets()


def kernel(nx, ny, src, cond, absn, out_ref, corr_ref, *s):
    (raw, obuf, cbuf, fxy, f0, f4, mass, inv, load, u0, u1, u2, pa, first, pb, ca, cb, last, tmp,
     cfxy, cf0, cf2, cmass, cinv, rl, cfirst, qa, qb, ra0, ra1, ra2, w0, w1, wa, wb, corr,
     s1, s2, s3, s4, ar1, ar2, arx, ary, sface, rface, scorner, rcorner,
     in_sem, out_sem, cout_sem, send_sem, recv_sem, ax_send, ax_recv, ay_send, ay_recv) = s
    x, y = lax.axis_index("gx"), lax.axis_index("gy")

    inputs = []
    for a, ref in enumerate((cond, absn, src)):
        for t in range(5):
            copy = pltpu.make_async_copy(ref.at[:, :, pl.ds(128 * t, 128)], raw.at[a, t], in_sem.at[a, t])
            copy.start()
            inputs.append(copy)

    def x_peer(d):
        return (lax.rem(x + d + nx, nx), y)

    def y_peer(d):
        return (x, lax.rem(y + d + ny, ny))

    barrier = pltpu.get_barrier_semaphore()
    greeted = [(lax.rem(x + dx + nx, nx), lax.rem(y + dy + ny, ny)) for dx, dy in DIRS[4:]]
    greeted += [x_peer(d) for d in range(1, nx)] + [y_peer(d) for d in range(1, ny)]
    for peer in greeted:
        pl.semaphore_signal(barrier, inc=1, device_id=peer, device_id_type=MESH)

    lf = Level(5, fxy, f0, f4, mass, inv)
    lc = Level(3, cfxy, cf0, cf2, cmass, cinv)
    bufs, sems, ids = (sface, rface, scorner, rcorner), (send_sem, recv_sem), (x, y, nx, ny)
    rounds = []

    def exchange(index, *fields):
        assert ROUNDS[index] == (sum(lv.q == 5 for lv, _ in fields), sum(lv.q == 3 for lv, _ in fields))
        e = Exchange(index, fields, OFFSETS[index], bufs, sems, ids)
        rounds.append(e)
        e.start()
        return e

    lanes = Lanes(5)

    def store_flux(i, j, p):
        put(f0, lf.edge(i, j), p[0])
        put(f4, lf.edge(i, j), p[4])
        put(fxy, lf.at(i, j, 0), p[0] + down(p[4]))
        for k in range(1, 4):
            put(fxy, lf.at(i, j, k), p[k])

    def store_plain(ref):
        def store(i, j, p):
            put(ref, lf.at(i, j, 0), p[0] + down(p[4]))
            for k in range(1, 4):
                put(ref, lf.at(i, j, k), p[k])

        return store

    for copy in inputs[:5]:
        copy.wait()
    load_field(lanes, raw.at[0], store_flux)
    for copy in inputs[5:10]:
        copy.wait()
    load_field(lanes, raw.at[1], store_plain(mass))
    for i in range(3):
        for j in range(3):
            ratio = WC[i] * WC[j] / (WF[2 * i] * WF[2 * j])
            ends, mid = ratio * WC[0] / WF[0], ratio * WC[1] / WF[2]
            put(cf0, lc.edge(i, j), ends * row(f0, lf.edge(2 * i, 2 * j)))
            put(cf2, lc.edge(i, j), ends * row(f4, lf.edge(2 * i, 2 * j)))
            for a, b in ((cfxy, fxy), (cmass, mass)):
                put(a, lc.at(i, j, 0), ends * row(b, lf.at(2 * i, 2 * j, 0)))
                put(a, lc.at(i, j, 1), mid * row(b, lf.at(2 * i, 2 * j, 2)))
    local_diag(lf, inv)
    local_diag(lc, cinv)

    pl.semaphore_wait(barrier, len(greeted))
    e_diag = exchange(0, (lf, inv), (lc, cinv))

    for copy in inputs[10:]:
        copy.wait()
    load_field(lanes, raw.at[2], store_plain(load))
    restrict_y(lf, load, tmp)
    join_planes_y(lf, load)
    join_planes_x(lf, load)
    restrict_xz(lc, tmp, rl)
    e_load = exchange(1, (lf, load), (lc, rl))

    def invert(lv):
        def body(i):
            for n in range(lv.q * lv.kz):
                p = lv.at(i, 0, 0) + n * 16
                put(lv.inv, p, 1.0 / row(lv.inv, p))

        lv.loop(lv.q, body)

    e_diag.finish()
    invert(lf)
    invert(lc)
    e_load.finish()

    apply_local(lf, pa, load)
    apply_local(lc, qa, rl)
    e_pa = exchange(2, (lf, pa), (lc, qa))
    apply_local(lf, ca, u0, scaled=load, restrict=tmp)
    restrict_xz(lc, tmp, ra0)
    e_ca = exchange(3, (lf, ca), (lc, ra0))
    e_pa.finish()
    apply_local(lf, pb, first, scaled=pa, sums=s1)
    apply_local(lc, qb, cfirst, scaled=qa, sums=s3)
    e_pb = exchange(4, (lf, pb), (lc, qb))
    e_ca.finish()
    apply_local(lf, cb, u1, scaled=ca, restrict=tmp)
    restrict_xz(lc, tmp, ra1)
    e_cb = exchange(5, (lf, cb), (lc, ra1))
    e_pb.finish()
    sum_squares(lf, pb, s2)
    sum_squares(lc, qb, s4)

    def fold(sums):
        return jnp.sum(sums[...], axis=0, keepdims=True)

    def to_all(source, slots, count, peer, send, recv):
        copies = []
        for d in range(1, count):
            copy = pltpu.make_async_remote_copy(
                src_ref=source, dst_ref=slots.at[d], send_sem=send.at[d], recv_sem=recv.at[d], device_id=peer(d), device_id_type=MESH
            )
            copy.start()
            copies.append(copy)
        return copies

    def gathered(source, slots, count, copies):
        for copy in copies:
            copy.wait_recv()
        total = source[...]
        for d in range(1, count):
            total = total + slots[d]
        return total

    ar1[...] = jnp.concatenate([fold(s1), fold(s2), fold(s3), fold(s4), jnp.zeros((4, 128), F32)], axis=0)
    x_copies = to_all(ar1, arx, nx, x_peer, ax_send, ax_recv)

    e_cb.finish()
    apply_local(lf, last, u2, scaled=cb, restrict=tmp, keep=False)
    restrict_xz(lc, tmp, ra2)
    e_ra2 = exchange(6, (lc, ra2))

    ar2[...] = gathered(ar1, arx, nx, x_copies)
    y_copies = to_all(ar2, ary, ny, y_peer, ay_send, ay_recv)
    e_ra2.finish()
    totals = jnp.sum(gathered(ar2, ary, ny, y_copies), axis=1, keepdims=True)

    def inverse_estimate(n):
        estimate = jnp.sqrt(totals[n + 1 : n + 2] / (totals[n : n + 1] + 1e-06))
        return jnp.broadcast_to(1.0 / estimate, (16, 128))

    g, gc = inverse_estimate(0), inverse_estimate(2)

    def horner(scale, a, b, c):
        return scale * (CHEB[0] * a + scale * (CHEB[1] * b + scale * (CHEB[2] * c)))

    for n in range(18):
        p = 16 * n
        put(wa, p, row(rl, p) - horner(g, row(ra0, p), row(ra1, p), row(ra2, p)))
    apply_local(lc, wb, w0, scaled=wa)
    e_w0 = exchange(7, (lc, wb))

    def smooth(i):
        for n in range(20):
            p = lf.at(i, 0, 0) + 16 * n
            put(u0, p, horner(g, row(u0, p), row(u1, p), row(u2, p)))

    loop(5, smooth)
    e_w0.finish()
    apply_local(lc, last, w1, scaled=wb)
    e_w1 = exchange(8, (lc, last))
    e_w1.finish()

    pieces3 = Lanes(3)
    copies = []
    for i in range(3):
        for j in range(3):
            for k in range(2):
                p = lc.at(i, j, k)
                w2 = row(last, p) * row(cinv, p)
                put(corr, p, horner(gc, row(w0, p), row(w1, p), w2))
            c = [row(corr, lc.at(i, j, 0)), row(corr, lc.at(i, j, 1))]
            c.append(up(c[0]))
            for h in range(2):
                stored = pieces3.merge([v[8 * h : 8 * h + 8] for v in c])
                for t in range(3):
                    cbuf[t, 6 * h + i, pl.ds(j, 4, 3), :] = stored[t][:4]
                    cbuf[t, 6 * h + 3 + i, pl.ds(j, 4, 3), :] = stored[t][4:]
    for t in range(3):
        copy = pltpu.make_async_copy(cbuf.at[t], corr_ref.at[:, :, pl.ds(128 * t, 128)], cout_sem.at[t])
        copy.start()
        copies.append(copy)

    for i in range(3):
        lines = []
        for j in range(3):
            a, b = row(corr, lc.at(i, j, 0)), row(corr, lc.at(i, j, 1))
            c = up(a)
            lines.append([a, JA * a + JB * b + JC * c, b, JC * a + JB * b + JA * c])
        for k in range(4):
            a, b, c = lines[0][k], lines[1][k], lines[2][k]
            for j, v in enumerate([a, JA * a + JB * b + JC * c, b, JC * a + JB * b + JA * c, c]):
                put(tmp, ((i * 5 + j) * 4 + k) * 16, v)

    def finish_plane(i):
        cx = [pick(i, [r[c] for r in JROWS]) for c in range(3)]
        for j in range(5):
            planes = []
            for k in range(4):
                lifted = [row(tmp, ((c * 5 + j) * 4 + k) * 16) for c in range(3)]
                lifted = cx[0] * lifted[0] + cx[1] * lifted[1] + cx[2] * lifted[2]
                planes.append(row(u0, lf.at(i, j, k)) + lifted)
            planes.append(up(planes[0]))
            for h in range(2):
                stored = lanes.merge([v[8 * h : 8 * h + 8] for v in planes])
                for t in range(5):
                    obuf[t, 10 * h + i, pl.ds(j, 4, 5), :] = stored[t][:4]
                    obuf[t, 10 * h + 5 + i, pl.ds(j, 4, 5), :] = stored[t][4:]

    loop(5, finish_plane)
    for t in range(5):
        copy = pltpu.make_async_copy(obuf.at[t], out_ref.at[:, :, pl.ds(128 * t, 128)], out_sem.at[t])
        copy.start()
        copies.append(copy)
    for e in rounds:
        e.wait_sent()
    for copy in x_copies + y_copies:
        copy.wait_send()
    for copy in copies:
        copy.wait()


def scratch(nx, ny):
    def v(*shape):
        return pltpu.VMEM(shape, F32)

    fine, coarse = v(FR, 128), v(CR, 128)
    dma = pltpu.SemaphoreType.DMA
    return (
        [v(3, 5, 20, 20, 128), v(5, 20, 20, 128), v(3, 12, 12, 128)]
        + [fine, v(ER, 128), v(ER, 128)]
        + [fine] * 12
        + [v(960, 128)]
        + [coarse, v(CER, 128), v(CER, 128)]
        + [coarse] * 14
        + [v(16, 128)] * 4
        + [v(8, 128), v(8, 128), v(nx, 8, 128), v(ny, 8, 128)]
        + [v(4, FACE_ROWS, 128)] * 2
        + [v(4, CORNER_ROWS, 128)] * 2
        + [dma((3, 5)), dma((5,)), dma((3,)), dma((len(ROUNDS), 8)), dma((len(ROUNDS), 8))]
        + [dma((nx,)), dma((nx,)), dma((ny,)), dma((ny,))]
    )


def solution(mesh):
    nx, ny = mesh.shape["gx"], mesh.shape["gy"]

    def on_device(source, conductivity, absorption):
        return pl.pallas_call(
            functools.partial(kernel, nx, ny),
            out_shape=(jax.ShapeDtypeStruct((20, 20, 640), F32), jax.ShapeDtypeStruct((12, 12, 384), F32)),
            in_specs=[pl.BlockSpec(memory_space=pl.ANY)] * 3,
            out_specs=[pl.BlockSpec(memory_space=pl.ANY)] * 2,
            scratch_shapes=scratch(nx, ny),
            compiler_params=pltpu.CompilerParams(collective_id=0, has_side_effects=True, vmem_limit_bytes=60 * 1024 * 1024),
            name="window",
        )(source, conductivity, absorption)

    placed = P("gx", "gy", None)
    return jax.shard_map(on_device, mesh=mesh, in_specs=(placed,) * 3, out_specs=(placed, placed), check_vma=False)
```

profile of v0, /device:TPU:1, one launch (start us, length us, event | category | flops | bytes accessed | tf_op | source)
XLA Modules:
  0.0 71.6 jit_solution(2592359405731783898)
XLA Ops:
  0.6 67.8 %window.1 = (f32[20,20,640]{2,1,0:T(8,128)}, f32[12,12,384]{2,1,0:T(8,128)}) custom-call(f32[20,20,640]{2,1,0:T(8,128)} %src.1, f32[20,20,640]{2,1,0:T(8,128)} %cond.1, f32[20,20,640]{2,1,0:T(8,128)} %absn.1), custom_call_target="tpu_custom_call" | custom-call | tf_op jit(solution)/shard_map/window/pallas_call | solution.py:809
  68.4 0.0 copy-start
  68.4 2.4 %copy.7 = f32[20,20,640]{2,1,0:T(8,128)} copy(f32[20,20,640]{2,1,0:T(8,128)} %get-tuple-element.4) | data formatting | bytes 2048000
  70.9 0.0 copy-done
  70.9 0.7 copy.8
Async XLA Ops:
  68.4 2.5 %copy-start = (f32[12,12,384]{2,1,0:T(8,128)S(1)}, f32[12,12,384]{2,1,0:T(8,128)}, u32[]{:S(2)}) copy-start(f32[12,12,384]{2,1,0:T(8,128)} %get-tuple-element.5) | copy-start | bytes 663556
where the time goes:
time: 71.7 us; the launch traced here: 71.6 us
  Pallas kernels  67.8 us (95%)
  local copies, waits for them, and re-layouts  3.16 us (4%)
    pallas_call x1, Pallas kernels, on_device(): pl.pallas_call(functools.partial(kernel, nx, ny), out_shape=(jax.ShapeDty...  67.8 us
    unnamed x4, local copies, waits for them, and re-layouts  3.16 us

commit v1 on v0

--- a/solution.py
+++ b/solution.py
@@ -106,12 +106,17 @@
     return pltpu.roll(x, 1, 1)
 
 
-def loop(count, body, unroll=1):
+def loop(count, body):
     def step(i, carry):
         body(i)
         return carry
 
-    lax.fori_loop(0, count, step, 0, unroll=unroll)
+    lax.fori_loop(0, count, step, 0)
+
+
+def unrolled(count, body):
+    for i in range(count):
+        body(i)
 
 
 class Level:
@@ -120,7 +125,6 @@
         self.fxy, self.f0, self.fq, self.mass, self.inv = fxy, f0, fq, mass, inv
         self.stiff, self.diag = (stiff5, diag5) if q == 5 else (stiff3, diag3)
         self.face = q * self.kz * 4
-        self.loop = loop if q == 5 else (lambda n, body: [body(i) for i in range(n)])
 
     def at(self, i, j, k):
         return ((i * self.q + j) * self.kz + k) * 16
@@ -167,7 +171,7 @@
             put(out, lv.at(0, j, k), lo)
             put(out, lv.at(q - 1, j, k), hi)
 
-    lv.loop(q, body)
+    unrolled(q, body)
 
 
 def join_planes_y(lv, out):
@@ -179,7 +183,7 @@
             put(out, lv.at(i, 0, k), lo)
             put(out, lv.at(i, q - 1, k), hi)
 
-    lv.loop(q, body)
+    unrolled(q, body)
 
 
 def apply_local(lv, out, u, scaled=None, sums=None, restrict=None, keep=True):
@@ -232,29 +236,24 @@
 
     if sums is not None:
         sums[...] = jnp.zeros_like(sums)
-    lv.loop(q, along_z)
-    lv.loop(q, along_x)
-    lv.loop(q, along_y)
+    unrolled(q, along_z)
+    unrolled(q, along_x)
+    unrolled(q, along_y)
     if keep:
         join_planes_x(lv, out)
 
 
 def sum_squares(lv, scaled, sums):
-    sums[...] = jnp.zeros_like(sums)
-
-    def body(i):
-        total = None
-        for j in range(lv.q):
+    total = [None] * 4
+    for i in range(lv.q - 1):
+        for j in range(lv.q - 1):
             for k in range(lv.kz):
                 p = lv.at(i, j, k)
                 v = row(scaled, p) * row(lv.inv, p)
                 v = v * v
-                if k == 0:
-                    v = v + v
-                total = v if total is None else total + v
-        sums[...] += total
-
-    lv.loop(lv.q, body)
+                zeros = (i == 0) + (j == 0) + (k == 0)
+                total[zeros] = v if total[zeros] is None else total[zeros] + v
+    sums[...] = total[0] + 2.0 * total[1] + 4.0 * total[2] + 8.0 * total[3]
 
 
 def restrict_xz(lc, tmp, out):
@@ -276,7 +275,7 @@
             for jc in range(3):
                 put(tmp, ((i * 3 + jc) * 4 + k) * 16, c[jc])
 
-    loop(5, body)
+    unrolled(5, body)
 
 
 def local_diag(lv, out):
@@ -307,9 +306,9 @@
             for j in range(q):
                 put(out, places[j], g[j])
 
-    lv.loop(q, along_z)
-    lv.loop(q, along_x)
-    lv.loop(q, along_y)
+    unrolled(q, along_z)
+    unrolled(q, along_x)
+    unrolled(q, along_y)
     join_planes_x(lv, out)
 
 
@@ -317,12 +316,13 @@
 
 
 class Exchange:
-    def __init__(self, round_index, fields, offsets, bufs, sems, ids):
+    def __init__(self, round_index, fields, offsets, bufs, sems, ids, forward):
         self.r, self.fields, self.ids = round_index, fields, ids
         self.face0, self.corner0 = offsets
         self.face_rows = sum(lv.face for lv, _ in fields)
         self.corner_rows = 8 * len(fields)
         self.bufs, self.sems = bufs, sems
+        self.dirs = [d for d, (dx, dy) in enumerate(DIRS) if not forward or (dx >= 0 and dy >= 0)]
         self.copies = []
 
     def pack(self):
@@ -331,6 +331,8 @@
         for f, (lv, ref) in enumerate(self.fields):
             q, kz = lv.q, lv.kz
             for d, (dx, dy) in enumerate(DIRS[:4]):
+                if d not in self.dirs:
+                    continue
                 if dy:
                     j, first = (q - 1, 3) if dy > 0 else (0, 0)
                     for i in range(q):
@@ -349,6 +351,8 @@
                             both = jnp.where(low, one, pltpu.roll(two, 4, 0))
                         sface[d, pl.ds(at + m * 4, 8), :] = both
             for c, (dx, dy) in enumerate(DIRS[4:]):
+                if c + 4 not in self.dirs:
+                    continue
                 p = lv.at(q - 1 if dx > 0 else 0, q - 1 if dy > 0 else 0, 0) + (12 if dx > 0 else 0) + (3 if dy > 0 else 0)
                 for k in range(kz):
                     scorner[c, pl.ds(self.corner0 + f * 8 + k, 1), :] = ref[pl.ds(p + 16 * k, 1), :]
@@ -358,7 +362,8 @@
         sface, rface, scorner, rcorner = self.bufs
         send_sem, recv_sem = self.sems
         x, y, nx, ny = self.ids
-        for d, (dx, dy) in enumerate(DIRS):
+        for d in self.dirs:
+            dx, dy = DIRS[d]
             if d < 4:
                 part = (d, pl.ds(self.face0, self.face_rows), slice(None))
                 src, dst = sface.at[part], rface.at[part]
@@ -388,6 +393,8 @@
         for f, (lv, ref) in enumerate(self.fields):
             q, kz = lv.q, lv.kz
             for d, (dx, dy) in enumerate(DIRS[:4]):
+                if d not in self.dirs:
+                    continue
                 if dy:
                     j, first = (0, 0) if dy > 0 else (q - 1, 3)
                     for i in range(q):
@@ -410,6 +417,8 @@
                             ref[a, :] = ref[a, :] + jnp.where(low, 0.0, turned)
                             ref[b, :] = ref[b, :] + jnp.where(low, 0.0, both)
             for c, (dx, dy) in enumerate(DIRS[4:]):
+                if c + 4 not in self.dirs:
+                    continue
                 p = lv.at(0 if dx > 0 else q - 1, 0 if dy > 0 else q - 1, 0) + (0 if dx > 0 else 12) + (0 if dy > 0 else 3)
                 for k in range(kz):
                     place = pl.ds(p + 16 * k, 1)
@@ -464,8 +473,7 @@
         )
         return lax.gather(x, index[..., None], numbers, slice_sizes=(1, 1), mode=lax.GatherScatterMode.PROMISE_IN_BOUNDS)
 
-    def split(self, stored):
-        moved = [self.gather(stored[t], self.split_index[t]) for t in range(self.q)]
+    def unmix(self, moved):
         out = []
         for k in range(self.q):
             x = moved[0]
@@ -474,14 +482,14 @@
             out.append(pltpu.roll(x, (128 - self.shift[k]) % 128, 1) if self.shift[k] else x)
         return out
 
-    def merge(self, nodes):
+    def mix(self, nodes):
         moved = [pltpu.roll(nodes[k], self.shift[k], 1) if self.shift[k] else nodes[k] for k in range(self.q)]
         out = []
         for t in range(self.q):
             x = moved[0]
             for k in range(1, self.q):
                 x = jnp.where(self.inside(k, t), moved[k], x)
-            out.append(self.gather(x, self.merge_index[t]))
+            out.append(x)
         return out
 
 
@@ -492,22 +500,29 @@
     return out
 
 
-def load_field(lanes, raw, store):
-    def body(i):
+def load_field(lanes, ref, raw, index, buf, sem, store):
+    def tile(t):
+        pltpu.make_async_copy(ref.at[:, :, pl.ds(pl.multiple_of(128 * t, 128), 128)], raw.at[t], sem.at[t]).wait()
+        order = index[t]
+        for i in range(5):
+            for j in range(5):
+                for h in range(2):
+                    low = raw[t, 10 * h + i, pl.ds(j, 4, 5), :]
+                    high = raw[t, 10 * h + 5 + i, pl.ds(j, 4, 5), :]
+                    both = jnp.concatenate([low, high], axis=0)
+                    buf[t, pl.ds((i * 5 + j) * 16 + 8 * h, 8), :] = lanes.gather(both, order)
+
+    def plane(i):
         wx = pick(i, WF)
         for j in range(5):
             halves = []
             for h in range(2):
-                stored = []
-                for t in range(5):
-                    low = raw[t, 10 * h + i, pl.ds(j, 4, 5), :]
-                    high = raw[t, 10 * h + 5 + i, pl.ds(j, 4, 5), :]
-                    stored.append(jnp.concatenate([low, high], axis=0))
-                halves.append(lanes.split(stored))
-            planes = [jnp.concatenate([halves[0][k], halves[1][k]], axis=0) * (wx * (WF[j] * WF[k])) for k in range(5)]
-            store(i, j, planes)
-
-    loop(5, body)
+                p = pl.ds(pl.multiple_of((i * 5 + j) * 16 + 8 * h, 8), 8)
+                halves.append(lanes.unmix([buf[t, p, :] for t in range(5)]))
+            store(i, j, [jnp.concatenate([halves[0][k], halves[1][k]], axis=0) * (wx * (WF[j] * WF[k])) for k in range(5)])
+
+    loop(5, tile)
+    loop(5, plane)
 
 
 FR, CR, ER, CER = 1600, 288, 400, 144
@@ -530,7 +545,7 @@
 
 CHEB = cheb_weights()
 
-ROUNDS = [(1, 1), (1, 1), (1, 1), (1, 1), (1, 1), (1, 1), (0, 1), (0, 1), (0, 1)]
+ROUNDS = [(1, 1), (1, 0), (0, 1), (1, 1), (1, 0), (1, 1), (1, 0), (0, 2), (0, 1), (0, 1), (0, 1)]
 
 
 def round_offsets():
@@ -545,19 +560,16 @@
 OFFSETS, FACE_ROWS, CORNER_ROWS = round_offsets()
 
 
-def kernel(nx, ny, src, cond, absn, out_ref, corr_ref, *s):
-    (raw, obuf, cbuf, fxy, f0, f4, mass, inv, load, u0, u1, u2, pa, first, pb, ca, cb, last, tmp,
-     cfxy, cf0, cf2, cmass, cinv, rl, cfirst, qa, qb, ra0, ra1, ra2, w0, w1, wa, wb, corr,
+def kernel(nx, ny, src, cond, absn, smooth_ref, corr, *s):
+    (raw, gbuf, split_index, fxy, f0, f4, mass, inv, load, u0, u1, u2, pa, first, pb, ca, cb, last, tmp,
+     cfxy, cf0, cf2, cmass, cinv, rl, cfirst, qa, qb, ra0, ra1, ra2, w0, w1, wa, wb, wc, base,
      s1, s2, s3, s4, ar1, ar2, arx, ary, sface, rface, scorner, rcorner,
-     in_sem, out_sem, cout_sem, send_sem, recv_sem, ax_send, ax_recv, ay_send, ay_recv) = s
+     in_sem, send_sem, recv_sem, ax_send, ax_recv, ay_send, ay_recv) = s
     x, y = lax.axis_index("gx"), lax.axis_index("gy")
 
-    inputs = []
-    for a, ref in enumerate((cond, absn, src)):
+    for a, ref in enumerate((src, cond, absn)):
         for t in range(5):
-            copy = pltpu.make_async_copy(ref.at[:, :, pl.ds(128 * t, 128)], raw.at[a, t], in_sem.at[a, t])
-            copy.start()
-            inputs.append(copy)
+            pltpu.make_async_copy(ref.at[:, :, pl.ds(128 * t, 128)], raw.at[a, t], in_sem.at[a, t]).start()
 
     def x_peer(d):
         return (lax.rem(x + d + nx, nx), y)
@@ -576,14 +588,19 @@
     bufs, sems, ids = (sface, rface, scorner, rcorner), (send_sem, recv_sem), (x, y, nx, ny)
     rounds = []
 
-    def exchange(index, *fields):
+    def exchange(index, *fields, forward=False):
         assert ROUNDS[index] == (sum(lv.q == 5 for lv, _ in fields), sum(lv.q == 3 for lv, _ in fields))
-        e = Exchange(index, fields, OFFSETS[index], bufs, sems, ids)
+        e = Exchange(index, fields, OFFSETS[index], bufs, sems, ids, forward)
         rounds.append(e)
         e.start()
         return e
 
     lanes = Lanes(5)
+    for t in range(5):
+        split_index[t] = lanes.split_index[t]
+
+    def read(a, ref, store):
+        load_field(lanes, ref, raw.at[a], split_index, gbuf, in_sem.at[a], store)
 
     def store_flux(i, j, p):
         put(f0, lf.edge(i, j), p[0])
@@ -600,12 +617,15 @@
 
         return store
 
-    for copy in inputs[:5]:
-        copy.wait()
-    load_field(lanes, raw.at[0], store_flux)
-    for copy in inputs[5:10]:
-        copy.wait()
-    load_field(lanes, raw.at[1], store_plain(mass))
+    read(0, src, store_plain(load))
+    restrict_y(lf, load, tmp)
+    join_planes_y(lf, load)
+    join_planes_x(lf, load)
+    restrict_xz(lc, tmp, rl)
+    read(1, cond, store_flux)
+    pl.semaphore_wait(barrier, len(greeted))
+    e_load = exchange(0, (lf, load), (lc, rl))
+    read(2, absn, store_plain(mass))
     for i in range(3):
         for j in range(3):
             ratio = WC[i] * WC[j] / (WF[2 * i] * WF[2 * j])
@@ -616,19 +636,9 @@
                 put(a, lc.at(i, j, 0), ends * row(b, lf.at(2 * i, 2 * j, 0)))
                 put(a, lc.at(i, j, 1), mid * row(b, lf.at(2 * i, 2 * j, 2)))
     local_diag(lf, inv)
+    e_diag = exchange(1, (lf, inv))
     local_diag(lc, cinv)
-
-    pl.semaphore_wait(barrier, len(greeted))
-    e_diag = exchange(0, (lf, inv), (lc, cinv))
-
-    for copy in inputs[10:]:
-        copy.wait()
-    load_field(lanes, raw.at[2], store_plain(load))
-    restrict_y(lf, load, tmp)
-    join_planes_y(lf, load)
-    join_planes_x(lf, load)
-    restrict_xz(lc, tmp, rl)
-    e_load = exchange(1, (lf, load), (lc, rl))
+    e_cdiag = exchange(2, (lc, cinv))
 
     def invert(lv):
         def body(i):
@@ -636,27 +646,28 @@
                 p = lv.at(i, 0, 0) + n * 16
                 put(lv.inv, p, 1.0 / row(lv.inv, p))
 
-        lv.loop(lv.q, body)
-
+        unrolled(lv.q, body)
+
+    e_load.finish()
+    apply_local(lf, pa, load)
+    apply_local(lc, qa, rl)
+    e_pa = exchange(3, (lf, pa), (lc, qa))
     e_diag.finish()
     invert(lf)
+    apply_local(lf, ca, u0, scaled=load, restrict=tmp)
+    e_ca = exchange(4, (lf, ca))
+    restrict_xz(lc, tmp, ra0)
+    e_cdiag.finish()
     invert(lc)
-    e_load.finish()
-
-    apply_local(lf, pa, load)
-    apply_local(lc, qa, rl)
-    e_pa = exchange(2, (lf, pa), (lc, qa))
-    apply_local(lf, ca, u0, scaled=load, restrict=tmp)
-    restrict_xz(lc, tmp, ra0)
-    e_ca = exchange(3, (lf, ca), (lc, ra0))
     e_pa.finish()
     apply_local(lf, pb, first, scaled=pa, sums=s1)
     apply_local(lc, qb, cfirst, scaled=qa, sums=s3)
-    e_pb = exchange(4, (lf, pb), (lc, qb))
+    e_pb = exchange(5, (lf, pb), (lc, qb), forward=True)
     e_ca.finish()
     apply_local(lf, cb, u1, scaled=ca, restrict=tmp)
+    e_cb = exchange(6, (lf, cb))
     restrict_xz(lc, tmp, ra1)
-    e_cb = exchange(5, (lf, cb), (lc, ra1))
+    e_ra01 = exchange(7, (lc, ra0), (lc, ra1))
     e_pb.finish()
     sum_squares(lf, pb, s2)
     sum_squares(lc, qb, s4)
@@ -688,10 +699,10 @@
     e_cb.finish()
     apply_local(lf, last, u2, scaled=cb, restrict=tmp, keep=False)
     restrict_xz(lc, tmp, ra2)
-    e_ra2 = exchange(6, (lc, ra2))
-
+    e_ra2 = exchange(8, (lc, ra2))
     ar2[...] = gathered(ar1, arx, nx, x_copies)
     y_copies = to_all(ar2, ary, ny, y_peer, ay_send, ay_recv)
+    e_ra01.finish()
     e_ra2.finish()
     totals = jnp.sum(gathered(ar2, ary, ny, y_copies), axis=1, keepdims=True)
 
@@ -708,43 +719,40 @@
         p = 16 * n
         put(wa, p, row(rl, p) - horner(g, row(ra0, p), row(ra1, p), row(ra2, p)))
     apply_local(lc, wb, w0, scaled=wa)
-    e_w0 = exchange(7, (lc, wb))
+    e_w0 = exchange(9, (lc, wb))
 
     def smooth(i):
         for n in range(20):
             p = lf.at(i, 0, 0) + 16 * n
-            put(u0, p, horner(g, row(u0, p), row(u1, p), row(u2, p)))
+            put(smooth_ref, p, horner(g, row(u0, p), row(u1, p), row(u2, p)))
 
     loop(5, smooth)
     e_w0.finish()
-    apply_local(lc, last, w1, scaled=wb)
-    e_w1 = exchange(8, (lc, last))
+    apply_local(lc, wc, w1, scaled=wb)
+    e_w1 = exchange(10, (lc, wc))
+    for n in range(18):
+        p = 16 * n
+        put(base, p, gc * (CHEB[0] * row(w0, p) + gc * (CHEB[1] * row(w1, p))))
     e_w1.finish()
-
-    pieces3 = Lanes(3)
-    copies = []
-    for i in range(3):
-        for j in range(3):
-            for k in range(2):
-                p = lc.at(i, j, k)
-                w2 = row(last, p) * row(cinv, p)
-                put(corr, p, horner(gc, row(w0, p), row(w1, p), w2))
-            c = [row(corr, lc.at(i, j, 0)), row(corr, lc.at(i, j, 1))]
-            c.append(up(c[0]))
-            for h in range(2):
-                stored = pieces3.merge([v[8 * h : 8 * h + 8] for v in c])
-                for t in range(3):
-                    cbuf[t, 6 * h + i, pl.ds(j, 4, 3), :] = stored[t][:4]
-                    cbuf[t, 6 * h + 3 + i, pl.ds(j, 4, 3), :] = stored[t][4:]
-    for t in range(3):
-        copy = pltpu.make_async_copy(cbuf.at[t], corr_ref.at[:, :, pl.ds(128 * t, 128)], cout_sem.at[t])
-        copy.start()
-        copies.append(copy)
+    for n in range(18):
+        p = 16 * n
+        put(corr, p, row(base, p) + gc * (gc * (gc * (CHEB[2] * row(wc, p) * row(cinv, p)))))
+
+    for e in rounds:
+        e.wait_sent()
+    for copy in x_copies + y_copies:
+        copy.wait_send()
+
+
+def lift(smooth_ref, corr, out_ref, corr_ref, gbuf, obuf, cbuf, merge_index, tmp, out_sem, cout_sem):
+    lanes = Lanes(5)
+    for t in range(5):
+        merge_index[t] = lanes.merge_index[t]
 
     for i in range(3):
         lines = []
         for j in range(3):
-            a, b = row(corr, lc.at(i, j, 0)), row(corr, lc.at(i, j, 1))
+            a, b = row(corr, ((i * 3 + j) * 2) * 16), row(corr, ((i * 3 + j) * 2 + 1) * 16)
             c = up(a)
             lines.append([a, JA * a + JB * b + JC * c, b, JC * a + JB * b + JA * c])
         for k in range(4):
@@ -759,23 +767,44 @@
             for k in range(4):
                 lifted = [row(tmp, ((c * 5 + j) * 4 + k) * 16) for c in range(3)]
                 lifted = cx[0] * lifted[0] + cx[1] * lifted[1] + cx[2] * lifted[2]
-                planes.append(row(u0, lf.at(i, j, k)) + lifted)
+                planes.append(row(smooth_ref, ((i * 5 + j) * 4 + k) * 16) + lifted)
             planes.append(up(planes[0]))
             for h in range(2):
-                stored = lanes.merge([v[8 * h : 8 * h + 8] for v in planes])
-                for t in range(5):
-                    obuf[t, 10 * h + i, pl.ds(j, 4, 5), :] = stored[t][:4]
-                    obuf[t, 10 * h + 5 + i, pl.ds(j, 4, 5), :] = stored[t][4:]
+                for t, v in enumerate(lanes.mix([v[8 * h : 8 * h + 8] for v in planes])):
+                    gbuf[t, pl.ds(pl.multiple_of((i * 5 + j) * 16 + 8 * h, 8), 8), :] = v
+
+    def out_copy(t):
+        return pltpu.make_async_copy(obuf.at[t], out_ref.at[:, :, pl.ds(pl.multiple_of(128 * t, 128), 128)], out_sem.at[t])
+
+    def finish_tile(t):
+        order = merge_index[t]
+        for i in range(5):
+            for j in range(5):
+                for h in range(2):
+                    stored = lanes.gather(gbuf[t, pl.ds((i * 5 + j) * 16 + 8 * h, 8), :], order)
+                    obuf[t, 10 * h + i, pl.ds(j, 4, 5), :] = stored[:4]
+                    obuf[t, 10 * h + 5 + i, pl.ds(j, 4, 5), :] = stored[4:]
+        out_copy(t).start()
 
     loop(5, finish_plane)
-    for t in range(5):
-        copy = pltpu.make_async_copy(obuf.at[t], out_ref.at[:, :, pl.ds(128 * t, 128)], out_sem.at[t])
+    loop(5, finish_tile)
+
+    thirds = Lanes(3)
+    for i in range(3):
+        for j in range(3):
+            c = [row(corr, ((i * 3 + j) * 2) * 16), row(corr, ((i * 3 + j) * 2 + 1) * 16)]
+            c.append(up(c[0]))
+            for h in range(2):
+                for t, v in enumerate(thirds.mix([v[8 * h : 8 * h + 8] for v in c])):
+                    stored = thirds.gather(v, thirds.merge_index[t])
+                    cbuf[t, 6 * h + i, pl.ds(j, 4, 3), :] = stored[:4]
+                    cbuf[t, 6 * h + 3 + i, pl.ds(j, 4, 3), :] = stored[4:]
+    copies = []
+    for t in range(3):
+        copy = pltpu.make_async_copy(cbuf.at[t], corr_ref.at[:, :, pl.ds(128 * t, 128)], cout_sem.at[t])
         copy.start()
         copies.append(copy)
-    for e in rounds:
-        e.wait_sent()
-    for copy in x_copies + y_copies:
-        copy.wait_send()
+    copies += [out_copy(t) for t in range(5)]
     for copy in copies:
         copy.wait()
 
@@ -787,17 +816,17 @@
     fine, coarse = v(FR, 128), v(CR, 128)
     dma = pltpu.SemaphoreType.DMA
     return (
-        [v(3, 5, 20, 20, 128), v(5, 20, 20, 128), v(3, 12, 12, 128)]
+        [v(3, 5, 20, 20, 128), v(5, 400, 128), pltpu.VMEM((5, 8, 128), jnp.int32)]
         + [fine, v(ER, 128), v(ER, 128)]
         + [fine] * 12
         + [v(960, 128)]
         + [coarse, v(CER, 128), v(CER, 128)]
-        + [coarse] * 14
+        + [coarse] * 15
         + [v(16, 128)] * 4
         + [v(8, 128), v(8, 128), v(nx, 8, 128), v(ny, 8, 128)]
         + [v(4, FACE_ROWS, 128)] * 2
         + [v(4, CORNER_ROWS, 128)] * 2
-        + [dma((3, 5)), dma((5,)), dma((3,)), dma((len(ROUNDS), 8)), dma((len(ROUNDS), 8))]
+        + [dma((3, 5)), dma((len(ROUNDS), 8)), dma((len(ROUNDS), 8))]
         + [dma((nx,)), dma((nx,)), dma((ny,)), dma((ny,))]
     )
 
@@ -806,15 +835,33 @@
     nx, ny = mesh.shape["gx"], mesh.shape["gy"]
 
     def on_device(source, conductivity, absorption):
-        return pl.pallas_call(
+        vmem, hbm = pl.BlockSpec(memory_space=pltpu.VMEM), pl.BlockSpec(memory_space=pltpu.HBM)
+        parts = pl.pallas_call(
             functools.partial(kernel, nx, ny),
-            out_shape=(jax.ShapeDtypeStruct((20, 20, 640), F32), jax.ShapeDtypeStruct((12, 12, 384), F32)),
-            in_specs=[pl.BlockSpec(memory_space=pl.ANY)] * 3,
-            out_specs=[pl.BlockSpec(memory_space=pl.ANY)] * 2,
+            out_shape=(jax.ShapeDtypeStruct((FR, 128), F32), jax.ShapeDtypeStruct((CR, 128), F32)),
+            in_specs=[hbm] * 3,
+            out_specs=[vmem] * 2,
             scratch_shapes=scratch(nx, ny),
-            compiler_params=pltpu.CompilerParams(collective_id=0, has_side_effects=True, vmem_limit_bytes=60 * 1024 * 1024),
+            compiler_params=pltpu.CompilerParams(collective_id=0, has_side_effects=True, vmem_limit_bytes=105 * 512 * 1024),
             name="window",
         )(source, conductivity, absorption)
+        return pl.pallas_call(
+            lift,
+            out_shape=(jax.ShapeDtypeStruct((20, 20, 640), F32), jax.ShapeDtypeStruct((12, 12, 384), F32)),
+            in_specs=[vmem] * 2,
+            out_specs=[hbm] * 2,
+            scratch_shapes=[
+                pltpu.VMEM((5, 400, 128), F32),
+                pltpu.VMEM((5, 20, 20, 128), F32),
+                pltpu.VMEM((3, 12, 12, 128), F32),
+                pltpu.VMEM((5, 8, 128), jnp.int32),
+                pltpu.VMEM((960, 128), F32),
+                pltpu.SemaphoreType.DMA((5,)),
+                pltpu.SemaphoreType.DMA((3,)),
+            ],
+            compiler_params=pltpu.CompilerParams(vmem_limit_bytes=16 * 1024 * 1024),
+            name="lift",
+        )(*parts)
 
     placed = P("gx", "gy", None)
     return jax.shard_map(on_device, mesh=mesh, in_specs=(placed,) * 3, out_specs=(placed, placed), check_vma=False)

time: 71.7 us -> 61.4 us (0.86)
  Pallas kernels: 67.8 us -> 60.6 us
  local copies, waits for them, and re-layouts: 3.16 us -> 0 us
    pallas_call x1, Pallas kernels: 67.8 us -> 58 us  [on_device(): pl.pallas_call(functools.partial(kernel, nx, ny), out_shape=(jax.ShapeDty...]
    unnamed x4 -> x0, local copies, waits for them, and re-layouts: 3.16 us -> none
    pallas_call x0 -> x1, Pallas kernels: none -> 2.6 us  [on_device(): pl.pallas_call(lift, out_shape=(jax.ShapeDtypeStruct((20, 20, 640), F32),...]
where the time goes in v1:
time: 61.4 us; the launch traced here: 61.3 us
  Pallas kernels  60.6 us (99%)
  between operations  0.64 us (1%)
    pallas_call x1, Pallas kernels, on_device(): pl.pallas_call(functools.partial(kernel, nx, ny), out_shape=(jax.ShapeDty...  58 us
    pallas_call x1, Pallas kernels, on_device(): pl.pallas_call(lift, out_shape=(jax.ShapeDtypeStruct((20, 20, 640), F32),...  2.6 us

profile of v1, /device:TPU:1, one launch (start us, length us, event | category | flops | bytes accessed | tf_op | source)
XLA Modules:
  0.0 61.3 jit_solution(15551049980102101526)
XLA Ops:
  0.6 58.0 %window.1 = (f32[1600,128]{1,0:T(8,128)S(1)}, f32[288,128]{1,0:T(8,128)S(1)}) custom-call(f32[20,20,640]{2,1,0:T(8,128)} %src.1, f32[20,20,640]{2,1,0:T(8,128)} %cond.1, f32[20,20,640]{2,1,0:T(8,128)} %absn.1), custom_call_target="tpu_custom_call" | custom-call | tf_op jit(solution)/shard_map/window/pallas_call | solution.py:839
  58.7 2.6 %lift.1 = (f32[20,20,640]{2,1,0:T(8,128)}, f32[12,12,384]{2,1,0:T(8,128)}) custom-call(f32[1600,128]{1,0:T(8,128)S(1)} %get-tuple-element.4.smooth_ref, f32[288,128]{1,0:T(8,128)S(1)} %get-tuple-element.5.corr), custom_call_target="tpu_custom_call" | custom-call | tf_op jit(solution)/shard_map/lift/pallas_call | solution.py:848

commit v2 on v1

--- a/solution.py
+++ b/solution.py
@@ -315,19 +315,30 @@
 DIRS = [(0, 1), (0, -1), (1, 0), (-1, 0), (1, 1), (1, -1), (-1, 1), (-1, -1)]
 
 
+def directions(forward):
+    return [d for d, (dx, dy) in enumerate(DIRS) if not forward or (dx >= 0 and dy >= 0)]
+
+
+def wait_all(ref, sem):
+    pltpu.make_async_copy(ref, ref, sem).wait()
+
+
 class Exchange:
-    def __init__(self, round_index, fields, offsets, bufs, sems, ids, forward):
+    def __init__(self, round_index, fields, region, bufs, sems, ids, forward):
         self.r, self.fields, self.ids = round_index, fields, ids
-        self.face0, self.corner0 = offsets
-        self.face_rows = sum(lv.face for lv, _ in fields)
-        self.corner_rows = 8 * len(fields)
         self.bufs, self.sems = bufs, sems
-        self.dirs = [d for d, (dx, dy) in enumerate(DIRS) if not forward or (dx >= 0 and dy >= 0)]
-        self.copies = []
+        face, corner = sum(lv.face for lv, _ in fields), 8 * len(fields)
+        self.dirs = directions(forward)
+        self.part, at = {}, region[0]
+        for d in self.dirs:
+            self.part[d] = (at, face if d < 4 else corner)
+            at += self.part[d][1]
+        assert at == region[0] + region[1]
+        self.region = pl.ds(*region)
 
     def pack(self):
-        sface, scorner = self.bufs[0], self.bufs[2]
-        at = self.face0
+        sbuf = self.bufs[0]
+        at = 0
         for f, (lv, ref) in enumerate(self.fields):
             q, kz = lv.q, lv.kz
             for d, (dx, dy) in enumerate(DIRS[:4]):
@@ -337,7 +348,7 @@
                     j, first = (q - 1, 3) if dy > 0 else (0, 0)
                     for i in range(q):
                         for h in range(0, 4 * kz, 8):
-                            sface[d, pl.ds(at + i * 4 * kz + h, 8), :] = ref[pl.ds(lv.at(i, j, 0) + first + 4 * h, 8, 4), :]
+                            sbuf[pl.ds(self.part[d][0] + at + i * 4 * kz + h, 8), :] = ref[pl.ds(lv.at(i, j, 0) + first + 4 * h, 8, 4), :]
                 else:
                     i = q - 1 if dx > 0 else 0
                     low = lax.broadcasted_iota(jnp.int32, (8, 128), 0) < 4
@@ -349,47 +360,39 @@
                         else:
                             one, two = ref[pl.ds(p, 8), :], ref[pl.ds(p + 16, 8), :]
                             both = jnp.where(low, one, pltpu.roll(two, 4, 0))
-                        sface[d, pl.ds(at + m * 4, 8), :] = both
+                        sbuf[pl.ds(self.part[d][0] + at + m * 4, 8), :] = both
             for c, (dx, dy) in enumerate(DIRS[4:]):
                 if c + 4 not in self.dirs:
                     continue
                 p = lv.at(q - 1 if dx > 0 else 0, q - 1 if dy > 0 else 0, 0) + (12 if dx > 0 else 0) + (3 if dy > 0 else 0)
                 for k in range(kz):
-                    scorner[c, pl.ds(self.corner0 + f * 8 + k, 1), :] = ref[pl.ds(p + 16 * k, 1), :]
+                    sbuf[pl.ds(self.part[c + 4][0] + f * 8 + k, 1), :] = ref[pl.ds(p + 16 * k, 1), :]
             at += lv.face
 
     def send(self):
-        sface, rface, scorner, rcorner = self.bufs
+        sbuf, rbuf = self.bufs
         send_sem, recv_sem = self.sems
         x, y, nx, ny = self.ids
         for d in self.dirs:
             dx, dy = DIRS[d]
-            if d < 4:
-                part = (d, pl.ds(self.face0, self.face_rows), slice(None))
-                src, dst = sface.at[part], rface.at[part]
-            else:
-                part = (d - 4, pl.ds(self.corner0, self.corner_rows), slice(None))
-                src, dst = scorner.at[part], rcorner.at[part]
-            copy = pltpu.make_async_remote_copy(
-                src_ref=src,
-                dst_ref=dst,
-                send_sem=send_sem.at[self.r, d],
-                recv_sem=recv_sem.at[self.r, d],
+            part = pl.ds(*self.part[d])
+            pltpu.make_async_remote_copy(
+                src_ref=sbuf.at[part],
+                dst_ref=rbuf.at[part],
+                send_sem=send_sem.at[self.r],
+                recv_sem=recv_sem.at[self.r],
                 device_id=(lax.rem(x + dx + nx, nx), lax.rem(y + dy + ny, ny)),
                 device_id_type=MESH,
-            )
-            copy.start()
-            self.copies.append(copy)
+            ).start()
 
     def start(self):
         self.pack()
         self.send()
 
     def finish(self):
-        for copy in self.copies:
-            copy.wait_recv()
-        rface, rcorner = self.bufs[1], self.bufs[3]
-        at = self.face0
+        rbuf = self.bufs[1]
+        wait_all(rbuf.at[self.region], self.sems[1].at[self.r])
+        at = 0
         for f, (lv, ref) in enumerate(self.fields):
             q, kz = lv.q, lv.kz
             for d, (dx, dy) in enumerate(DIRS[:4]):
@@ -400,13 +403,13 @@
                     for i in range(q):
                         for h in range(0, 4 * kz, 8):
                             place = pl.ds(lv.at(i, j, 0) + first + 4 * h, 8, 4)
-                            ref[place, :] = ref[place, :] + rface[d, pl.ds(at + i * 4 * kz + h, 8), :]
+                            ref[place, :] = ref[place, :] + rbuf[pl.ds(self.part[d][0] + at + i * 4 * kz + h, 8), :]
                 else:
                     i = 0 if dx > 0 else q - 1
                     low = lax.broadcasted_iota(jnp.int32, (8, 128), 0) < 4
                     for m in range(0, q * kz, 2):
                         p = lv.at(i, 0, 0) + m * 16
-                        both = rface[d, pl.ds(at + m * 4, 8), :]
+                        both = rbuf[pl.ds(self.part[d][0] + at + m * 4, 8), :]
                         turned = pltpu.roll(both, 4, 0)
                         if dx > 0:
                             a, b = pl.ds(p, 8), pl.ds(p + 16, 8)
@@ -422,12 +425,11 @@
                 p = lv.at(0 if dx > 0 else q - 1, 0 if dy > 0 else q - 1, 0) + (0 if dx > 0 else 12) + (0 if dy > 0 else 3)
                 for k in range(kz):
                     place = pl.ds(p + 16 * k, 1)
-                    ref[place, :] = ref[place, :] + rcorner[c, pl.ds(self.corner0 + f * 8 + k, 1), :]
+                    ref[place, :] = ref[place, :] + rbuf[pl.ds(self.part[c + 4][0] + f * 8 + k, 1), :]
             at += lv.face
 
     def wait_sent(self):
-        for copy in self.copies:
-            copy.wait_send()
+        wait_all(self.bufs[0].at[self.region], self.sems[0].at[self.r])
 
 
 class Lanes:
@@ -545,26 +547,28 @@
 
 CHEB = cheb_weights()
 
-ROUNDS = [(1, 1), (1, 0), (0, 1), (1, 1), (1, 0), (1, 1), (1, 0), (0, 2), (0, 1), (0, 1), (0, 1)]
-
-
-def round_offsets():
-    face, corner, out = 0, 0, []
-    for fine, coarse in ROUNDS:
-        out.append((face, corner))
-        face += 80 * fine + 24 * coarse
-        corner += 8 * (fine + coarse)
-    return out, face, corner
-
-
-OFFSETS, FACE_ROWS, CORNER_ROWS = round_offsets()
-
-
-def kernel(nx, ny, src, cond, absn, smooth_ref, corr, *s):
+ROUNDS = [
+    (1, 0, False), (1, 0, False), (0, 2, False), (1, 0, False), (1, 0, False), (0, 1, False), (1, 0, True), (0, 2, False),
+    (0, 1, True), (1, 0, False), (0, 1, False), (0, 1, False), (0, 2, False), (0, 1, False), (0, 1, False),
+]
+
+
+def round_regions():
+    at, out = 0, []
+    for fine, coarse, forward in ROUNDS:
+        sizes = [80 * fine + 24 * coarse if d < 4 else 8 * (fine + coarse) for d in directions(forward)]
+        out.append((at, sum(sizes)))
+        at += sum(sizes)
+    return out, at
+
+
+REGIONS, BUF_ROWS = round_regions()
+
+
+def kernel(nx, ny, src, cond, absn, smooth_ref, corr, merge_index, *s):
     (raw, gbuf, split_index, fxy, f0, f4, mass, inv, load, u0, u1, u2, pa, first, pb, ca, cb, last, tmp,
-     cfxy, cf0, cf2, cmass, cinv, rl, cfirst, qa, qb, ra0, ra1, ra2, w0, w1, wa, wb, wc, base,
-     s1, s2, s3, s4, ar1, ar2, arx, ary, sface, rface, scorner, rcorner,
-     in_sem, send_sem, recv_sem, ax_send, ax_recv, ay_send, ay_recv) = s
+     cfxy, cf0, cf2, cmass, cinv, rl, cfirst, qa, qb, ra0, ra1, ra2, vl, v0, v1, v2, al, a0, a1, a2, w0, w1, wa, wc, base,
+     s1, s2, s3, s4, ar1, ar2, arx, ary, sbuf, rbuf, in_sem, send_sem, recv_sem, ar_send, ar_recv) = s
     x, y = lax.axis_index("gx"), lax.axis_index("gy")
 
     for a, ref in enumerate((src, cond, absn)):
@@ -585,19 +589,21 @@
 
     lf = Level(5, fxy, f0, f4, mass, inv)
     lc = Level(3, cfxy, cf0, cf2, cmass, cinv)
-    bufs, sems, ids = (sface, rface, scorner, rcorner), (send_sem, recv_sem), (x, y, nx, ny)
+    bufs, sems, ids = (sbuf, rbuf), (send_sem, recv_sem), (x, y, nx, ny)
     rounds = []
 
     def exchange(index, *fields, forward=False):
-        assert ROUNDS[index] == (sum(lv.q == 5 for lv, _ in fields), sum(lv.q == 3 for lv, _ in fields))
-        e = Exchange(index, fields, OFFSETS[index], bufs, sems, ids, forward)
+        e = Exchange(index, fields, REGIONS[index], bufs, sems, ids, forward)
+        e.start()
+        if len(rounds) >= 4:
+            rounds[-4].wait_sent()
         rounds.append(e)
-        e.start()
         return e
 
     lanes = Lanes(5)
     for t in range(5):
         split_index[t] = lanes.split_index[t]
+        merge_index[t] = lanes.merge_index[t]
 
     def read(a, ref, store):
         load_field(lanes, ref, raw.at[a], split_index, gbuf, in_sem.at[a], store)
@@ -624,7 +630,7 @@
     restrict_xz(lc, tmp, rl)
     read(1, cond, store_flux)
     pl.semaphore_wait(barrier, len(greeted))
-    e_load = exchange(0, (lf, load), (lc, rl))
+    e_load = exchange(0, (lf, load))
     read(2, absn, store_plain(mass))
     for i in range(3):
         for j in range(3):
@@ -638,7 +644,7 @@
     local_diag(lf, inv)
     e_diag = exchange(1, (lf, inv))
     local_diag(lc, cinv)
-    e_cdiag = exchange(2, (lc, cinv))
+    e_coarse = exchange(2, (lc, rl), (lc, cinv))
 
     def invert(lv):
         def body(i):
@@ -650,61 +656,75 @@
 
     e_load.finish()
     apply_local(lf, pa, load)
-    apply_local(lc, qa, rl)
-    e_pa = exchange(3, (lf, pa), (lc, qa))
+    e_pa = exchange(3, (lf, pa))
     e_diag.finish()
     invert(lf)
     apply_local(lf, ca, u0, scaled=load, restrict=tmp)
     e_ca = exchange(4, (lf, ca))
     restrict_xz(lc, tmp, ra0)
-    e_cdiag.finish()
+    e_coarse.finish()
     invert(lc)
+    apply_local(lc, qa, rl)
+    e_qa = exchange(5, (lc, qa))
+    apply_local(lc, al, vl, scaled=rl)
     e_pa.finish()
     apply_local(lf, pb, first, scaled=pa, sums=s1)
+    e_pb = exchange(6, (lf, pb), forward=True)
+    e_al = exchange(7, (lc, ra0), (lc, al))
+    e_qa.finish()
     apply_local(lc, qb, cfirst, scaled=qa, sums=s3)
-    e_pb = exchange(5, (lf, pb), (lc, qb), forward=True)
+    e_qb = exchange(8, (lc, qb), forward=True)
     e_ca.finish()
     apply_local(lf, cb, u1, scaled=ca, restrict=tmp)
-    e_cb = exchange(6, (lf, cb))
+    e_cb = exchange(9, (lf, cb))
     restrict_xz(lc, tmp, ra1)
-    e_ra01 = exchange(7, (lc, ra0), (lc, ra1))
     e_pb.finish()
     sum_squares(lf, pb, s2)
+    e_qb.finish()
     sum_squares(lc, qb, s4)
 
     def fold(sums):
         return jnp.sum(sums[...], axis=0, keepdims=True)
 
-    def to_all(source, slots, count, peer, send, recv):
-        copies = []
+    def to_all(phase, source, slots, count, peer):
         for d in range(1, count):
-            copy = pltpu.make_async_remote_copy(
-                src_ref=source, dst_ref=slots.at[d], send_sem=send.at[d], recv_sem=recv.at[d], device_id=peer(d), device_id_type=MESH
-            )
-            copy.start()
-            copies.append(copy)
-        return copies
-
-    def gathered(source, slots, count, copies):
-        for copy in copies:
-            copy.wait_recv()
+            pltpu.make_async_remote_copy(
+                src_ref=source,
+                dst_ref=slots.at[d],
+                send_sem=ar_send.at[phase],
+                recv_sem=ar_recv.at[phase],
+                device_id=peer(d),
+                device_id_type=MESH,
+            ).start()
+
+    def gathered(phase, source, slots, count):
+        wait_all(slots.at[pl.ds(1, count - 1)], ar_recv.at[phase])
         total = source[...]
         for d in range(1, count):
             total = total + slots[d]
+        wait_all(slots.at[pl.ds(1, count - 1)], ar_send.at[phase])
         return total
 
     ar1[...] = jnp.concatenate([fold(s1), fold(s2), fold(s3), fold(s4), jnp.zeros((4, 128), F32)], axis=0)
-    x_copies = to_all(ar1, arx, nx, x_peer, ax_send, ax_recv)
+    to_all(0, ar1, arx, nx, x_peer)
+    e_ra1 = exchange(10, (lc, ra1))
+    e_al.finish()
+    apply_local(lc, a0, v0, scaled=ra0)
 
     e_cb.finish()
     apply_local(lf, last, u2, scaled=cb, restrict=tmp, keep=False)
     restrict_xz(lc, tmp, ra2)
-    e_ra2 = exchange(8, (lc, ra2))
-    ar2[...] = gathered(ar1, arx, nx, x_copies)
-    y_copies = to_all(ar2, ary, ny, y_peer, ay_send, ay_recv)
-    e_ra01.finish()
+    e_ra2 = exchange(11, (lc, ra2))
+    e_ra1.finish()
+    apply_local(lc, a1, v1, scaled=ra1)
+    ar2[...] = gathered(0, ar1, arx, nx)
+    to_all(1, ar2, ary, ny, y_peer)
+    e_a01 = exchange(12, (lc, a0), (lc, a1))
     e_ra2.finish()
-    totals = jnp.sum(gathered(ar2, ary, ny, y_copies), axis=1, keepdims=True)
+    apply_local(lc, a2, v2, scaled=ra2)
+    e_a2 = exchange(13, (lc, a2))
+    e_a01.finish()
+    totals = jnp.sum(gathered(1, ar2, ary, ny), axis=1, keepdims=True)
 
     def inverse_estimate(n):
         estimate = jnp.sqrt(totals[n + 1 : n + 2] / (totals[n : n + 1] + 1e-06))
@@ -717,9 +737,8 @@
 
     for n in range(18):
         p = 16 * n
-        put(wa, p, row(rl, p) - horner(g, row(ra0, p), row(ra1, p), row(ra2, p)))
-    apply_local(lc, wb, w0, scaled=wa)
-    e_w0 = exchange(9, (lc, wb))
+        put(w0, p, row(vl, p) - horner(g, row(v0, p), row(v1, p), row(v2, p)))
+        put(wa, p, row(al, p) - g * (CHEB[0] * row(a0, p) + g * (CHEB[1] * row(a1, p))))
 
     def smooth(i):
         for n in range(20):
@@ -727,9 +746,12 @@
             put(smooth_ref, p, horner(g, row(u0, p), row(u1, p), row(u2, p)))
 
     loop(5, smooth)
-    e_w0.finish()
-    apply_local(lc, wc, w1, scaled=wb)
-    e_w1 = exchange(10, (lc, wc))
+    e_a2.finish()
+    for n in range(18):
+        p = 16 * n
+        put(wa, p, row(wa, p) - g * (g * (g * (CHEB[2] * row(a2, p)))))
+    apply_local(lc, wc, w1, scaled=wa)
+    e_w1 = exchange(14, (lc, wc))
     for n in range(18):
         p = 16 * n
         put(base, p, gc * (CHEB[0] * row(w0, p) + gc * (CHEB[1] * row(w1, p))))
@@ -738,16 +760,12 @@
         p = 16 * n
         put(corr, p, row(base, p) + gc * (gc * (gc * (CHEB[2] * row(wc, p) * row(cinv, p)))))
 
-    for e in rounds:
+    for e in rounds[-4:]:
         e.wait_sent()
-    for copy in x_copies + y_copies:
-        copy.wait_send()
-
-
-def lift(smooth_ref, corr, out_ref, corr_ref, gbuf, obuf, cbuf, merge_index, tmp, out_sem, cout_sem):
+
+
+def lift(smooth_ref, corr, merge_index, out_ref, corr_ref, gbuf, obuf, cbuf, tmp, out_sem, cout_sem):
     lanes = Lanes(5)
-    for t in range(5):
-        merge_index[t] = lanes.merge_index[t]
 
     for i in range(3):
         lines = []
@@ -821,13 +839,11 @@
         + [fine] * 12
         + [v(960, 128)]
         + [coarse, v(CER, 128), v(CER, 128)]
-        + [coarse] * 15
+        + [coarse] * 22
         + [v(16, 128)] * 4
         + [v(8, 128), v(8, 128), v(nx, 8, 128), v(ny, 8, 128)]
-        + [v(4, FACE_ROWS, 128)] * 2
-        + [v(4, CORNER_ROWS, 128)] * 2
-        + [dma((3, 5)), dma((len(ROUNDS), 8)), dma((len(ROUNDS), 8))]
-        + [dma((nx,)), dma((nx,)), dma((ny,)), dma((ny,))]
+        + [v(BUF_ROWS, 128)] * 2
+        + [dma((3, 5)), dma((len(ROUNDS),)), dma((len(ROUNDS),)), dma((2,)), dma((2,))]
     )
 
 
@@ -838,9 +854,9 @@
         vmem, hbm = pl.BlockSpec(memory_space=pltpu.VMEM), pl.BlockSpec(memory_space=pltpu.HBM)
         parts = pl.pallas_call(
             functools.partial(kernel, nx, ny),
-            out_shape=(jax.ShapeDtypeStruct((FR, 128), F32), jax.ShapeDtypeStruct((CR, 128), F32)),
+            out_shape=(jax.ShapeDtypeStruct((FR, 128), F32), jax.ShapeDtypeStruct((CR, 128), F32), jax.ShapeDtypeStruct((5, 8, 128), jnp.int32)),
             in_specs=[hbm] * 3,
-            out_specs=[vmem] * 2,
+            out_specs=[vmem] * 3,
             scratch_shapes=scratch(nx, ny),
             compiler_params=pltpu.CompilerParams(collective_id=0, has_side_effects=True, vmem_limit_bytes=105 * 512 * 1024),
             name="window",
@@ -848,13 +864,12 @@
         return pl.pallas_call(
             lift,
             out_shape=(jax.ShapeDtypeStruct((20, 20, 640), F32), jax.ShapeDtypeStruct((12, 12, 384), F32)),
-            in_specs=[vmem] * 2,
+            in_specs=[vmem] * 3,
             out_specs=[hbm] * 2,
             scratch_shapes=[
                 pltpu.VMEM((5, 400, 128), F32),
                 pltpu.VMEM((5, 20, 20, 128), F32),
                 pltpu.VMEM((3, 12, 12, 128), F32),
-                pltpu.VMEM((5, 8, 128), jnp.int32),
                 pltpu.VMEM((960, 128), F32),
                 pltpu.SemaphoreType.DMA((5,)),
                 pltpu.SemaphoreType.DMA((3,)),

time: 61.4 us -> 55.1 us (0.90)
  Pallas kernels: 60.6 us -> 54.4 us
    pallas_call x1, Pallas kernels: 58 us -> 51.8 us  [on_device(): pl.pallas_call(functools.partial(kernel, nx, ny), out_shape=(jax.ShapeDty...]
where the time goes in v2:
time: 55.1 us; the launch traced here: 55 us
  Pallas kernels  54.4 us (99%)
  between operations  0.64 us (1%)
    pallas_call x1, Pallas kernels, on_device(): pl.pallas_call(functools.partial(kernel, nx, ny), out_shape=(jax.ShapeDty...  51.8 us
    pallas_call x1, Pallas kernels, on_device(): pl.pallas_call(lift, out_shape=(jax.ShapeDtypeStruct((20, 20, 640), F32),...  2.6 us

profile of v2, /device:TPU:1, one launch (start us, length us, event | category | flops | bytes accessed | tf_op | source)
XLA Modules:
  0.0 55.0 jit_solution(8139792869541699201)
XLA Ops:
  0.6 51.8 %window.1 = (f32[1600,128]{1,0:T(8,128)S(1)}, f32[288,128]{1,0:T(8,128)S(1)}, s32[5,8,128]{2,1,0:T(8,128)S(1)}) custom-call(f32[20,20,640]{2,1,0:T(8,128)} %src.1, f32[20,20,640]{2,1,0:T(8,128)} %cond.1, f32[20,20,640]{2,1,0:T(8,128)} %absn.1), custom_call_target="tpu_custom_call" | custom-call | tf_op jit(solution)/shard_map/window/pallas_call | solution.py:855
  52.4 2.6 %lift.1 = (f32[20,20,640]{2,1,0:T(8,128)}, f32[12,12,384]{2,1,0:T(8,128)}) custom-call(f32[1600,128]{1,0:T(8,128)S(1)} %get-tuple-element.5.smooth_ref, f32[288,128]{1,0:T(8,128)S(1)} %get-tuple-element.6.corr, s32[5,8,128]{2,1,0:T(8,128)S(1)} %get-tuple-element.7.merge_index), custom_call_target="tpu_custom_call" | custom-call | tf_op jit(solution)/shard_map/lift/pallas_call | solution.py:864

commit v3 on v2

--- a/solution.py
+++ b/solution.py
@@ -767,46 +767,6 @@
 def lift(smooth_ref, corr, merge_index, out_ref, corr_ref, gbuf, obuf, cbuf, tmp, out_sem, cout_sem):
     lanes = Lanes(5)
 
-    for i in range(3):
-        lines = []
-        for j in range(3):
-            a, b = row(corr, ((i * 3 + j) * 2) * 16), row(corr, ((i * 3 + j) * 2 + 1) * 16)
-            c = up(a)
-            lines.append([a, JA * a + JB * b + JC * c, b, JC * a + JB * b + JA * c])
-        for k in range(4):
-            a, b, c = lines[0][k], lines[1][k], lines[2][k]
-            for j, v in enumerate([a, JA * a + JB * b + JC * c, b, JC * a + JB * b + JA * c, c]):
-                put(tmp, ((i * 5 + j) * 4 + k) * 16, v)
-
-    def finish_plane(i):
-        cx = [pick(i, [r[c] for r in JROWS]) for c in range(3)]
-        for j in range(5):
-            planes = []
-            for k in range(4):
-                lifted = [row(tmp, ((c * 5 + j) * 4 + k) * 16) for c in range(3)]
-                lifted = cx[0] * lifted[0] + cx[1] * lifted[1] + cx[2] * lifted[2]
-                planes.append(row(smooth_ref, ((i * 5 + j) * 4 + k) * 16) + lifted)
-            planes.append(up(planes[0]))
-            for h in range(2):
-                for t, v in enumerate(lanes.mix([v[8 * h : 8 * h + 8] for v in planes])):
-                    gbuf[t, pl.ds(pl.multiple_of((i * 5 + j) * 16 + 8 * h, 8), 8), :] = v
-
-    def out_copy(t):
-        return pltpu.make_async_copy(obuf.at[t], out_ref.at[:, :, pl.ds(pl.multiple_of(128 * t, 128), 128)], out_sem.at[t])
-
-    def finish_tile(t):
-        order = merge_index[t]
-        for i in range(5):
-            for j in range(5):
-                for h in range(2):
-                    stored = lanes.gather(gbuf[t, pl.ds((i * 5 + j) * 16 + 8 * h, 8), :], order)
-                    obuf[t, 10 * h + i, pl.ds(j, 4, 5), :] = stored[:4]
-                    obuf[t, 10 * h + 5 + i, pl.ds(j, 4, 5), :] = stored[4:]
-        out_copy(t).start()
-
-    loop(5, finish_plane)
-    loop(5, finish_tile)
-
     thirds = Lanes(3)
     for i in range(3):
         for j in range(3):
@@ -822,6 +782,47 @@
         copy = pltpu.make_async_copy(cbuf.at[t], corr_ref.at[:, :, pl.ds(128 * t, 128)], cout_sem.at[t])
         copy.start()
         copies.append(copy)
+
+    for i in range(3):
+        lines = []
+        for j in range(3):
+            a, b = row(corr, ((i * 3 + j) * 2) * 16), row(corr, ((i * 3 + j) * 2 + 1) * 16)
+            c = up(a)
+            lines.append([a, JA * a + JB * b + JC * c, b, JC * a + JB * b + JA * c])
+        for k in range(4):
+            a, b, c = lines[0][k], lines[1][k], lines[2][k]
+            for j, v in enumerate([a, JA * a + JB * b + JC * c, b, JC * a + JB * b + JA * c, c]):
+                put(tmp, ((i * 5 + j) * 4 + k) * 16, v)
+
+    def finish_plane(i):
+        cx = [pick(i, [r[c] for r in JROWS]) for c in range(3)]
+        for j in range(5):
+            planes = []
+            for k in range(4):
+                lifted = [row(tmp, ((c * 5 + j) * 4 + k) * 16) for c in range(3)]
+                lifted = cx[0] * lifted[0] + cx[1] * lifted[1] + cx[2] * lifted[2]
+                planes.append(row(smooth_ref, ((i * 5 + j) * 4 + k) * 16) + lifted)
+            planes.append(up(planes[0]))
+            for h in range(2):
+                for t, v in enumerate(lanes.mix([v[8 * h : 8 * h + 8] for v in planes])):
+                    gbuf[t, pl.ds(pl.multiple_of((i * 5 + j) * 16 + 8 * h, 8), 8), :] = v
+
+    def out_copy(t):
+        return pltpu.make_async_copy(obuf.at[t], out_ref.at[:, :, pl.ds(pl.multiple_of(128 * t, 128), 128)], out_sem.at[t])
+
+    def finish_tile(t):
+        order = merge_index[t]
+        for i in range(5):
+            for j in range(5):
+                for h in range(2):
+                    stored = lanes.gather(gbuf[t, pl.ds((i * 5 + j) * 16 + 8 * h, 8), :], order)
+                    obuf[t, 10 * h + i, pl.ds(j, 4, 5), :] = stored[:4]
+                    obuf[t, 10 * h + 5 + i, pl.ds(j, 4, 5), :] = stored[4:]
+        out_copy(t).start()
+
+    loop(5, finish_plane)
+    loop(5, finish_tile)
+
     copies += [out_copy(t) for t in range(5)]
     for copy in copies:
         copy.wait()

time: 55.1 us -> 55 us (level)
  no operation moved by 1% of the time
where the time goes in v3:
time: 55 us; the launch traced here: 54.9 us
  Pallas kernels  54.3 us (99%)
  between operations  0.64 us (1%)
    pallas_call x1, Pallas kernels, on_device(): pl.pallas_call(functools.partial(kernel, nx, ny), out_shape=(jax.ShapeDty...  51.8 us
    pallas_call x1, Pallas kernels, on_device(): pl.pallas_call(lift, out_shape=(jax.ShapeDtypeStruct((20, 20, 640), F32),...  2.5 us

profile of v3, /device:TPU:1, one launch (start us, length us, event | category | flops | bytes accessed | tf_op | source)
XLA Modules:
  0.0 54.9 jit_solution(15118947641003510985)
XLA Ops:
  0.6 51.8 %window.1 = (f32[1600,128]{1,0:T(8,128)S(1)}, f32[288,128]{1,0:T(8,128)S(1)}, s32[5,8,128]{2,1,0:T(8,128)S(1)}) custom-call(f32[20,20,640]{2,1,0:T(8,128)} %src.1, f32[20,20,640]{2,1,0:T(8,128)} %cond.1, f32[20,20,640]{2,1,0:T(8,128)} %absn.1), custom_call_target="tpu_custom_call" | custom-call | tf_op jit(solution)/shard_map/window/pallas_call | solution.py:856
  52.4 2.5 %lift.1 = (f32[20,20,640]{2,1,0:T(8,128)}, f32[12,12,384]{2,1,0:T(8,128)}) custom-call(f32[1600,128]{1,0:T(8,128)S(1)} %get-tuple-element.5.smooth_ref, f32[288,128]{1,0:T(8,128)S(1)} %get-tuple-element.6.corr, s32[5,8,128]{2,1,0:T(8,128)S(1)} %get-tuple-element.7.merge_index), custom_call_target="tpu_custom_call" | custom-call | tf_op jit(solution)/shard_map/lift/pallas_call | solution.py:865
